TPU v7x, 32 devices: a whole 2x2x4 slice. The times are simulated.
32 devices in a mesh: gx: 4 (over y, x), gy: 2 (over core), gz: 4 (over z).
Axes of the slice: x: 2, y: 2, z: 4, core: 2. Of those that a mesh axis runs over, the one named last changes fastest.
Arguments:
- measures: float32 [65536, 256], P(('gx', 'gy', 'gz')), may hold values from -6 to 6
- group_index: int32 [65536], P(('gx', 'gy', 'gz')), may hold values from 0 to 511, as said below
- distinct_keys: int32 [32, 512], P(('gx', 'gy', 'gz')), may hold values from 32 to 65567, as said below
- group_counts: int32 [32], P(('gx', 'gy', 'gz')), may hold values from 128 to 512, as said below
Outputs:
- group_sums: float32 [16384, 256], P(('gx', 'gy', 'gz'))
- group_rows: int32 [16384], P(('gx', 'gy', 'gz'))
- group_keys: int32 [16384], P(('gx', 'gy', 'gz'))
- group_total: int32 [], replicated
Inputs may be any that keep to these rules, and one draw needn't show every extreme that they name: `group_counts`: every device has between 128 and 512 groups, and some device has exactly 512. `group_index`: each row's index lies below its device's group count, and every group of a device has at least one row. `distinct_keys`: each device's keys rise strictly; all keys of device d equal d modulo 32, so no key lives on two devices; entries at and past the device's count are unused.
All inputs are finite; a program needn't handle non-finite values.
Results may differ from a plain program's by a relative error of at most 0.0003.
Values sent between devices are 32-bit elements; how exact they have to be, the bound alone decides.
A program may use at most 64 MiB of HBM per device.

v0:
```python
import jax
import jax.numpy as jnp
from jax import lax
from jax.sharding import PartitionSpec as P


def shards(measures, group_index, distinct_keys, group_counts):
    rows, width = measures.shape
    span = distinct_keys.shape[1]
    devices = lax.axis_size(("gx", "gy", "gz"))
    slots = span // devices
    plane = lax.axis_size("gx") * lax.axis_size("gy")
    line = lax.axis_size("gz")
    count = group_counts[0]
    myself = jnp.int32(0)
    sender_counts = lax.all_gather(group_counts, ("gx", "gy", "gz"), axis=0, tiled=True)
    sender_offsets = jnp.cumsum(sender_counts) - sender_counts
    myself = lax.axis_index(("gx", "gy", "gz"))
    offset = sender_offsets[myself]
    group_total = jnp.sum(sender_counts)
    block = min(1024, rows)
    labels = lax.broadcasted_iota(jnp.int32, (span, block), 0)

    def accumulate(step, carry):
        totals, tallies = carry
        start = step * block
        index = lax.dynamic_slice_in_dim(group_index, start, block)
        values = lax.dynamic_slice_in_dim(measures, start, block, 0)
        hits = index[None, :] == labels
        totals = totals + jnp.dot(
            hits.astype(jnp.float32),
            values,
            precision=lax.Precision.HIGHEST,
            preferred_element_type=jnp.float32,
        )
        tallies = tallies + jnp.sum(hits, axis=1, dtype=jnp.int32)
        return (totals, tallies)

    sums, tallies = lax.fori_loop(
        0,
        rows // block,
        accumulate,
        (jnp.zeros((span, width), jnp.float32), jnp.zeros((span,), jnp.int32)),
    )
    local = jnp.arange(span, dtype=jnp.int32)
    live = local < count
    keys = jnp.where(live, distinct_keys[0], -1)
    fields = jnp.stack([tallies.astype(jnp.float32), keys.astype(jnp.float32)], axis=1)
    extra = fields.shape[1]

    def arrange(array):
        shaped = array.reshape((slots, devices) + array.shape[1:])
        rolled = jnp.roll(shaped, offset, axis=1)
        return rolled.reshape((slots, plane, line) + array.shape[1:])

    outgoing = (arrange(sums), arrange(fields))
    arrived = (
        lax.all_to_all(
            lax.all_to_all(outgoing[0], "gz", split_axis=2, concat_axis=2, tiled=True),
            ("gx", "gy"),
            split_axis=1,
            concat_axis=1,
            tiled=True,
        ),
        lax.all_to_all(
            lax.all_to_all(outgoing[1], "gz", split_axis=2, concat_axis=2, tiled=True),
            ("gx", "gy"),
            split_axis=1,
            concat_axis=1,
            tiled=True,
        ),
    )
    got_sums, got_fields = arrived
    got_fields = got_fields.reshape(-1, extra)
    sender = jnp.arange(devices, dtype=jnp.int32).reshape(1, plane, line)
    start_of = sender_offsets.reshape(1, plane, line)
    count_of = sender_counts.reshape(1, plane, line)
    level = jnp.arange(slots, dtype=jnp.int32).reshape(slots, 1, 1)
    position = level * devices + (myself - start_of) % devices
    arrived_live = (position < count_of) & (sender >= 0)
    target = jnp.where(arrived_live, (start_of + position) // devices, span).reshape(-1)
    group_sums = (
        jnp.zeros((span, width), jnp.float32)
        .at[target]
        .set(got_sums.reshape(-1, width), mode="drop")
    )
    group_rows = (
        jnp.zeros((span,), jnp.int32)
        .at[target]
        .set(got_fields[:, 0].astype(jnp.int32), mode="drop")
    )
    group_keys = (
        jnp.full((span,), -1, jnp.int32)
        .at[target]
        .set(got_fields[:, 1].astype(jnp.int32), mode="drop")
    )
    return (group_sums, group_rows, group_keys, group_total)


def solution(mesh):
    return jax.shard_map(
        shards,
        mesh=mesh,
        in_specs=(
            P(("gx", "gy", "gz"), None),
            P(("gx", "gy", "gz")),
            P(("gx", "gy", "gz"), None),
            P(("gx", "gy", "gz")),
        ),
        out_specs=(P(("gx", "gy", "gz"), None), P(("gx", "gy", "gz")), P(("gx", "gy", "gz")), P()),
        check_vma=False,
    )
```

profile of v0, /device:TPU:0, one launch (start us, length us, event | category | flops | bytes accessed | tf_op | source)
XLA Modules:
  0.0 106.3 jit_solution(15189355763401430567)
XLA Ops:
  1.3 0.1 dynamic-update-slice
  1.4 42.0 %all-reduce = s32[32]{0:T(128)S(1)} all-reduce(s32[32]{0:T(128)S(1)} %dynamic-update-slice), channel_id=1, replica_groups=mesh['gx'=4,'gy'=2,'gz'=4] {'gx','gy','gz'}, use_global_device_ids=true, to_apply=%add | all-reduce | flops 32 | bytes 256
  43.4 0.1 copy.37
  43.5 0.1 reduce.1
  43.6 0.6 fusion.19
  44.3 0.6 dynamic_slice.25
  46.8 7.4 %while.16 = (s32[]{:T(128)}, f32[512,256]{1,0:T(8,128)S(1)}, s32[512]{0:T(512)S(1)}, s32[2048]{0:T(1024)}, f32[2048,256]{1,0:T(8,128)}, /*index=5*/s32[]{:T(128)}, s32[]{:T(128)}, s32[]{:T(128)}, s32[]{:T(128)}) while((s32[]{:T(128)}, f32[512,256]{1,0:T(8,128)S(1)}, s32[512]{0:T(512)S(1)}, s32[2048]{0:T(1024)}, ...), condition=%wide.region_3.4_spmd.clone, body=%wide.region_1.3_spmd.clone.sunk | while | flops 1612972544 | bytes 2121886 | solution.py:39
  46.9 0.7 dynamic_slice.55
  47.6 2.7 %fusion.24 = f32[512,256]{1,0:T(8,128)S(1)} fusion(f32[2048,256]{1,0:T(8,128)} %get-tuple-element.203, s32[]{:T(128)S(6)} %select_n.107, s32[1024]{0:T(1024)S(1)} %dynamic_slice.55, f32[512,256]{1,0:T(8,128)S(1)} %get-tuple-element.191, pred[]{:T(512)S(6)} %compare.20), kind=kOutput, calls=%fused_computation.8.clone.1 | convolution fusion | flops 1611399168 | bytes 2101253 | tf_op jit(solution)/shard_map/while/body/eval_jaxpr/dot_general | solution.py:30
  50.2 0.3 fusion.25
  50.6 0.7 dynamic_slice.55
  51.2 2.7 %fusion.24 = f32[512,256]{1,0:T(8,128)S(1)} fusion(f32[2048,256]{1,0:T(8,128)} %get-tuple-element.203, s32[]{:T(128)S(6)} %select_n.107, s32[1024]{0:T(1024)S(1)} %dynamic_slice.55, f32[512,256]{1,0:T(8,128)S(1)} %get-tuple-element.191, pred[]{:T(512)S(6)} %compare.20), kind=kOutput, calls=%fused_computation.8.clone.1 | convolution fusion | flops 1611399168 | bytes 2101253 | tf_op jit(solution)/shard_map/while/body/eval_jaxpr/dot_general | solution.py:30
  53.9 0.3 fusion.25
  54.3 0.5 broadcast.199
  54.8 0.7 reduce.5
  55.5 0.1 squeeze.13
  55.6 0.1 fusion.13
  55.7 0.1 copy.42
  55.8 0.7 reshape.312
  56.5 3.6 %all-to-all-start.2 = ((f32[4,1,256]{2,1,0:T(1,128)}), f32[4,1,256]{2,1,0:T(1,128)S(1)}, u32[]{:S(2)}, u32[]{:S(2)}) async-start(f32[4,1,256]{2,1,0:T(1,128)} %reshape.312), calls=%async_computation.2 | async-start | bytes 8192 | tf_op jit(solution)/shard_map/all_to_all | solution.py:66
  60.1 0.1 fusion.9
  60.2 0.3 copy.38
  60.5 1.1 %copy.39 = f32[16,8,4,256]{3,1,0,2:T(8,128)} copy(f32[16,8,4,256]{3,0,2,1:T(8,128)S(1)} %bitcast.23) | data formatting | bytes 1048576 | tf_op jit(solution)/shard_map/reshape | solution.py:54
  61.6 4.0 %all-to-all-done.2 = f32[4,1,256]{2,1,0:T(1,128)S(1)} async-done(((f32[4,1,256]{2,1,0:T(1,128)}), f32[4,1,256]{2,1,0:T(1,128)S(1)}, u32[]{:S(2)}, u32[]{:S(2)}) %all-to-all-start.2) | async-done | bytes 4128 | tf_op jit(solution)/shard_map/all_to_all | solution.py:66
  65.6 3.5 %all-to-all-start = ((f32[16,8,4,256]{3,1,0,2:T(8,128)}), f32[16,8,4,256]{3,1,0,2:T(8,128)S(1)}, u32[]{:S(2)}, u32[]{:S(2)}) async-start(f32[16,8,4,256]{3,1,0,2:T(8,128)} %copy.39), calls=%async_computation | async-start | bytes 1048576 | tf_op jit(solution)/shard_map/all_to_all | solution.py:59
  69.1 0.1 reshape.258
  69.2 0.1 add_add_fusion
  69.3 0.5 broadcast.200
  69.8 0.7 reduce.6
  70.5 0.1 reshape.313
  70.6 0.7 reshape.314
  71.3 10.3 %all-to-all-done = f32[16,8,4,256]{3,1,0,2:T(8,128)S(1)} async-done(((f32[16,8,4,256]{3,1,0,2:T(8,128)}), f32[16,8,4,256]{3,1,0,2:T(8,128)S(1)}, u32[]{:S(2)}, u32[]{:S(2)}) %all-to-all-start) | async-done | bytes 524320 | tf_op jit(solution)/shard_map/all_to_all | solution.py:59
  81.6 3.6 %all-to-all-start.3 = ((f32[8,1,128]{2,1,0:T(1,128)}), f32[8,1,128]{2,1,0:T(1,128)S(1)}, u32[]{:S(2)}, u32[]{:S(2)}) async-start(f32[8,1,128]{2,1,0:T(1,128)} %reshape.314), calls=%async_computation.3 | async-start | bytes 8192 | tf_op jit(solution)/shard_map/all_to_all | solution.py:65
  85.2 1.1 %copy.40 = f32[16,8,4,256]{3,2,0,1:T(4,128)} copy(f32[16,8,4,256]{3,1,0,2:T(8,128)S(1)} %all-to-all-done) | data formatting | bytes 1048576 | tf_op jit(solution)/shard_map/all_to_all | solution.py:59
  86.4 3.5 %all-to-all-done.3 = f32[8,1,128]{2,1,0:T(1,128)S(1)} async-done(((f32[8,1,128]{2,1,0:T(1,128)}), f32[8,1,128]{2,1,0:T(1,128)S(1)}, u32[]{:S(2)}, u32[]{:S(2)}) %all-to-all-start.3) | async-done | bytes 4128 | tf_op jit(solution)/shard_map/all_to_all | solution.py:65
  89.8 3.5 %all-to-all-start.1 = ((f32[16,8,4,256]{3,2,0,1:T(4,128)}), f32[16,8,4,256]{3,2,0,1:T(4,128)S(1)}, u32[]{:S(2)}, u32[]{:S(2)}) async-start(f32[16,8,4,256]{3,2,0,1:T(4,128)} %copy.40), calls=%async_computation.1 | async-start | bytes 1048576 | tf_op jit(solution)/shard_map/all_to_all | solution.py:58
  93.3 0.1 fusion.12
  93.4 0.1 add.155
  93.5 0.1 and.67
  93.7 0.7 reduce.7
  94.4 0.1 reshape.315
  94.5 0.2 copy.45
  94.6 0.1 reshape.266
  94.8 3.0 %scatter_custom_fusion.1 = s32[512]{0:T(512)} fusion(s32[512]{0:T(512)S(1)} %bitcast.30, s32[512]{0:T(512)S(1)} %bitcast.34, s32[]{:T(128)} %constant.107.clone.1), kind=kCustom, calls=%fused_computation.40 | custom fusion | bytes 2052 | tf_op jit(solution)/shard_map/scatter | solution.py:90
  97.8 3.0 %scatter_custom_fusion.2 = s32[512]{0:T(512)} fusion(s32[512]{0:T(512)S(1)} %bitcast.31, s32[512]{0:T(512)S(1)} %bitcast.33, s32[]{:T(128)} %constant.111.clone.1), kind=kCustom, calls=%fused_computation.38 | custom fusion | bytes 2052 | tf_op jit(solution)/shard_map/scatter | solution.py:95
  100.8 2.2 %all-to-all-done.1 = f32[16,8,4,256]{3,2,0,1:T(4,128)S(1)} async-done(((f32[16,8,4,256]{3,2,0,1:T(4,128)}), f32[16,8,4,256]{3,2,0,1:T(4,128)S(1)}, u32[]{:S(2)}, u32[]{:S(2)}) %all-to-all-start.1) | async-done | bytes 524320 | tf_op jit(solution)/shard_map/all_to_all | solution.py:58
  103.0 0.2 reshape.271
  103.2 3.0 %scatter_custom_fusion = f32[512,256]{1,0:T(8,128)} fusion(s32[512]{0:T(512)S(1)} %bitcast.32, f32[512,256]{1,0:T(8,128)S(1)} %reshape.271, f32[]{:T(128)} %constant.100.clone.1), kind=kCustom, calls=%fused_computation.16 | custom fusion | bytes 524292 | tf_op jit(solution)/shard_map/scatter | solution.py:85
  (20 shorter events, 0.4 us)
Async XLA Ops:
  46.8 8.0 %copy-start = (s32[1,512]{1,0:T(1,128)S(1)}, s32[1,512]{1,0:T(1,128)}, u32[]{:S(2)}) copy-start(s32[1,512]{1,0:T(1,128)} %param.8) | copy-start | bytes 6148
  56.5 9.2 %all-to-all-start.2 = ((f32[4,1,256]{2,1,0:T(1,128)}), f32[4,1,256]{2,1,0:T(1,128)S(1)}, u32[]{:S(2)}, u32[]{:S(2)}) async-start(f32[4,1,256]{2,1,0:T(1,128)} %reshape.312), calls=%async_computation.2 | async-start | bytes 8192 | tf_op jit(solution)/shard_map/all_to_all | solution.py:66
  65.6 16.0 %all-to-all-start = ((f32[16,8,4,256]{3,1,0,2:T(8,128)}), f32[16,8,4,256]{3,1,0,2:T(8,128)S(1)}, u32[]{:S(2)}, u32[]{:S(2)}) async-start(f32[16,8,4,256]{3,1,0,2:T(8,128)} %copy.39), calls=%async_computation | async-start | bytes 1048576 | tf_op jit(solution)/shard_map/all_to_all | solution.py:59
  81.6 8.2 %all-to-all-start.3 = ((f32[8,1,128]{2,1,0:T(1,128)}), f32[8,1,128]{2,1,0:T(1,128)S(1)}, u32[]{:S(2)}, u32[]{:S(2)}) async-start(f32[8,1,128]{2,1,0:T(1,128)} %reshape.314), calls=%async_computation.3 | async-start | bytes 8192 | tf_op jit(solution)/shard_map/all_to_all | solution.py:65
  89.8 13.2 %all-to-all-start.1 = ((f32[16,8,4,256]{3,2,0,1:T(4,128)}), f32[16,8,4,256]{3,2,0,1:T(4,128)S(1)}, u32[]{:S(2)}, u32[]{:S(2)}) async-start(f32[16,8,4,256]{3,2,0,1:T(4,128)} %copy.40), calls=%async_computation.1 | async-start | bytes 1048576 | tf_op jit(solution)/shard_map/all_to_all | solution.py:58
where the time goes:
time: 107 us; the launch traced here: 106 us
  blocking collectives  42 us (39%)
  waiting for transfers between devices  20.1 us (19%)
  local copies, waits for them, and re-layouts  17.5 us (16%)
  starting transfers between devices  14.1 us (13%)
  matrix products  5.34 us (5%)
  other arithmetic  3.86 us (4%)
  between operations  3.41 us (3%)
    unnamed x1, blocking collectives  42 us
    all_to_all x1, waiting for transfers between devices, shards(): lax.all_to_all(outgoing[0], 'gz', split_axis=2, concat_axis=2, tiled=True)  10.3 us
    dot_general x2, matrix products, accumulate(): jnp.dot(hits.astype(jnp.float32), values, precision=lax.Precision.HIGHEST...  5.34 us
    all_to_all x1, waiting for transfers between devices, shards(): lax.all_to_all(outgoing[1], 'gz', split_axis=2, concat_axis=2, tiled=True)  4.02 us
    all_to_all x1, starting transfers between devices, shards(): lax.all_to_all(outgoing[1], 'gz', split_axis=2, concat_axis=2, tiled=True)  3.6 us
    all_to_all x1, starting transfers between devices, shards(): lax.all_to_all(lax.all_to_all(outgoing[1], 'gz', split_axis=2, concat_axi...  3.56 us
    all_to_all x1, starting transfers between devices, shards(): lax.all_to_all(lax.all_to_all(outgoing[0], 'gz', split_axis=2, concat_axi...  3.49 us
    all_to_all x1, starting transfers between devices, shards(): lax.all_to_all(outgoing[0], 'gz', split_axis=2, concat_axis=2, tiled=True)  3.47 us
  transfers between devices with their start and end apart: 4, of which 4 were waited for; matrix products, arithmetic and copies ran while one was open for 12% of the time, Pallas kernels for 0%

commit v1 on v0

--- a/solution.py
+++ b/solution.py
@@ -62,12 +62,20 @@
             concat_axis=1,
             tiled=True,
         ),
-        lax.all_to_all(
-            lax.all_to_all(outgoing[1], "gz", split_axis=2, concat_axis=2, tiled=True),
-            ("gx", "gy"),
-            split_axis=1,
-            concat_axis=1,
-            tiled=True,
+        jnp.concatenate(
+            lax.all_to_all(
+                jnp.stack(
+                    jnp.split(
+                        lax.all_to_all(outgoing[1], "gz", split_axis=2, concat_axis=2, tiled=True),
+                        lax.axis_size(("gx", "gy")),
+                        axis=1,
+                    )
+                ),
+                ("gx", "gy"),
+                0,
+                0,
+            ),
+            axis=1,
         ),
     )
     got_sums, got_fields = arrived

time: 107 us -> 107 us (level)
    unnamed x9 -> x16, local copies, waits for them, and re-layouts: 2.18 us -> 2.24 us
where the time goes in v1:
time: 107 us; the launch traced here: 106 us
  blocking collectives  41.9 us (39%)
  waiting for transfers between devices  19.9 us (19%)
  local copies, waits for them, and re-layouts  17.5 us (16%)
  starting transfers between devices  14.1 us (13%)
  matrix products  5.34 us (5%)
  other arithmetic  3.85 us (4%)
  between operations  3.45 us (3%)
    unnamed x1, blocking collectives  41.9 us
    all_to_all x1, waiting for transfers between devices, shards(): lax.all_to_all(outgoing[0], 'gz', split_axis=2, concat_axis=2, tiled=True)  10.4 us
    dot_general x2, matrix products, accumulate(): jnp.dot(hits.astype(jnp.float32), values, precision=lax.Precision.HIGHEST...  5.34 us
    all_to_all x1, waiting for transfers between devices, shards(): lax.all_to_all(outgoing[1], 'gz', split_axis=2, concat_axis=2, tiled=True)  3.74 us
    all_to_all x1, starting transfers between devices, shards(): lax.all_to_all(outgoing[1], 'gz', split_axis=2, concat_axis=2, tiled=True)  3.59 us
    all_to_all x1, starting transfers between devices, shards(): lax.all_to_all(jnp.stack(jnp.split(lax.all_to_all(outgoing[1], 'gz', spli...  3.55 us
    all_to_all x1, starting transfers between devices, shards(): lax.all_to_all(lax.all_to_all(outgoing[0], 'gz', split_axis=2, concat_axi...  3.49 us
    all_to_all x1, starting transfers between devices, shards(): lax.all_to_all(outgoing[0], 'gz', split_axis=2, concat_axis=2, tiled=True)  3.47 us
  transfers between devices with their start and end apart: 4, of which 4 were waited for; matrix products, arithmetic and copies ran while one was open for 12% of the time, Pallas kernels for 0%

profile of v1, /device:TPU:0, one launch (start us, length us, event | category | flops | bytes accessed | tf_op | source)
XLA Modules:
  0.0 106.2 jit_solution(10687705699491854767)
XLA Ops:
  1.3 0.1 dynamic-update-slice
  1.4 41.9 %all-reduce = s32[32]{0:T(128)S(1)} all-reduce(s32[32]{0:T(128)S(1)} %dynamic-update-slice), channel_id=1, replica_groups=mesh['gx'=4,'gy'=2,'gz'=4] {'gx','gy','gz'}, use_global_device_ids=true, to_apply=%add | all-reduce | flops 32 | bytes 256
  43.4 0.1 copy.58
  43.5 0.1 reduce.1
  43.6 0.6 fusion.20
  44.3 0.6 dynamic_slice.25
  46.8 7.4 %while.16 = (s32[]{:T(128)}, f32[512,256]{1,0:T(8,128)S(1)}, s32[512]{0:T(512)S(1)}, s32[2048]{0:T(1024)}, f32[2048,256]{1,0:T(8,128)}, /*index=5*/s32[]{:T(128)}, s32[]{:T(128)}, s32[]{:T(128)}, s32[]{:T(128)}) while((s32[]{:T(128)}, f32[512,256]{1,0:T(8,128)S(1)}, s32[512]{0:T(512)S(1)}, s32[2048]{0:T(1024)}, ...), condition=%wide.region_3.4_spmd.clone, body=%wide.region_1.3_spmd.clone.sunk | while | flops 1612972544 | bytes 2121894 | solution.py:39
  46.8 0.7 dynamic_slice.55
  47.5 2.7 %fusion.25 = f32[512,256]{1,0:T(8,128)S(1)} fusion(f32[2048,256]{1,0:T(8,128)} %get-tuple-element.211, s32[]{:T(128)S(6)} %select_n.107, s32[1024]{0:T(1024)S(1)} %dynamic_slice.55, f32[512,256]{1,0:T(8,128)S(1)} %get-tuple-element.199, pred[]{:T(512)S(6)} %compare.20), kind=kOutput, calls=%fused_computation.8.clone.1 | convolution fusion | flops 1611399168 | bytes 2101253 | tf_op jit(solution)/shard_map/while/body/eval_jaxpr/dot_general | solution.py:30
  50.2 0.3 fusion.26
  50.5 0.7 dynamic_slice.55
  51.2 2.7 %fusion.25 = f32[512,256]{1,0:T(8,128)S(1)} fusion(f32[2048,256]{1,0:T(8,128)} %get-tuple-element.211, s32[]{:T(128)S(6)} %select_n.107, s32[1024]{0:T(1024)S(1)} %dynamic_slice.55, f32[512,256]{1,0:T(8,128)S(1)} %get-tuple-element.199, pred[]{:T(512)S(6)} %compare.20), kind=kOutput, calls=%fused_computation.8.clone.1 | convolution fusion | flops 1611399168 | bytes 2101253 | tf_op jit(solution)/shard_map/while/body/eval_jaxpr/dot_general | solution.py:30
  53.9 0.3 fusion.26
  54.2 0.5 broadcast.199
  54.7 0.7 reduce.5
  55.4 0.1 squeeze.13
  55.5 0.1 stack.34
  55.6 0.1 fusion.13
  55.7 0.7 reshape.312
  56.4 3.6 %all-to-all-start.2 = ((f32[4,1,256]{2,1,0:T(1,128)}), f32[4,1,256]{2,1,0:T(1,128)S(1)}, u32[]{:S(2)}, u32[]{:S(2)}) async-start(f32[4,1,256]{2,1,0:T(1,128)} %reshape.312), calls=%async_computation.2 | async-start | bytes 8192 | tf_op jit(solution)/shard_map/all_to_all | solution.py:69
  60.1 0.1 fusion.9
  60.3 0.1 add_add_fusion
  60.4 0.1 lt.86
  60.5 0.3 copy.59
  60.8 1.1 %copy.60 = f32[16,8,4,256]{3,1,0,2:T(8,128)} copy(f32[16,8,4,256]{3,0,2,1:T(8,128)S(1)} %bitcast.40) | data formatting | bytes 1048576 | tf_op jit(solution)/shard_map/reshape | solution.py:54
  61.9 3.7 %all-to-all-done.2 = f32[4,1,256]{2,1,0:T(1,128)S(1)} async-done(((f32[4,1,256]{2,1,0:T(1,128)}), f32[4,1,256]{2,1,0:T(1,128)S(1)}, u32[]{:S(2)}, u32[]{:S(2)}) %all-to-all-start.2) | async-done | bytes 4128 | tf_op jit(solution)/shard_map/all_to_all | solution.py:69
  65.6 3.5 %all-to-all-start = ((f32[16,8,4,256]{3,1,0,2:T(8,128)}), f32[16,8,4,256]{3,1,0,2:T(8,128)S(1)}, u32[]{:S(2)}, u32[]{:S(2)}) async-start(f32[16,8,4,256]{3,1,0,2:T(8,128)} %copy.60), calls=%async_computation | async-start | bytes 1048576 | tf_op jit(solution)/shard_map/all_to_all | solution.py:59
  69.1 0.5 broadcast.200
  69.6 0.7 reduce.6
  70.3 0.1 reshape.313
  70.5 0.7 reshape.314
  71.2 10.4 %all-to-all-done = f32[16,8,4,256]{3,1,0,2:T(8,128)S(1)} async-done(((f32[16,8,4,256]{3,1,0,2:T(8,128)}), f32[16,8,4,256]{3,1,0,2:T(8,128)S(1)}, u32[]{:S(2)}, u32[]{:S(2)}) %all-to-all-start) | async-done | bytes 524320 | tf_op jit(solution)/shard_map/all_to_all | solution.py:59
  81.6 3.6 %all-to-all-start.3 = ((f32[8,1,128]{2,1,0:T(1,128)}), f32[8,1,128]{2,1,0:T(1,128)S(1)}, u32[]{:S(2)}, u32[]{:S(2)}) async-start(f32[8,1,128]{2,1,0:T(1,128)} %reshape.314), calls=%async_computation.3 | async-start | bytes 8192 | tf_op jit(solution)/shard_map/all_to_all | solution.py:66
  85.1 0.1 fusion.12
  85.2 0.1 and.67
  85.3 0.1 add.155
  85.5 1.1 %copy.61 = f32[16,8,4,256]{3,2,0,1:T(4,128)} copy(f32[16,8,4,256]{3,1,0,2:T(8,128)S(1)} %all-to-all-done) | data formatting | bytes 1048576 | tf_op jit(solution)/shard_map/all_to_all | solution.py:59
  86.6 3.2 %all-to-all-done.3 = f32[8,1,128]{2,1,0:T(1,128)S(1)} async-done(((f32[8,1,128]{2,1,0:T(1,128)}), f32[8,1,128]{2,1,0:T(1,128)S(1)}, u32[]{:S(2)}, u32[]{:S(2)}) %all-to-all-start.3) | async-done | bytes 4128 | tf_op jit(solution)/shard_map/all_to_all | solution.py:66
  89.8 3.5 %all-to-all-start.1 = ((f32[16,8,4,256]{3,2,0,1:T(4,128)}), f32[16,8,4,256]{3,2,0,1:T(4,128)S(1)}, u32[]{:S(2)}, u32[]{:S(2)}) async-start(f32[16,8,4,256]{3,2,0,1:T(4,128)} %copy.61), calls=%async_computation.1 | async-start | bytes 1048576 | tf_op jit(solution)/shard_map/all_to_all | solution.py:58
  93.4 0.7 reduce.7
  94.0 0.1 reshape.315
  94.1 0.2 copy.73
  94.3 0.1 reshape_reshape.3
  94.4 3.0 %scatter_custom_fusion.1 = s32[512]{0:T(512)} fusion(s32[512]{0:T(512)S(1)} %bitcast.46, s32[512]{0:T(512)S(1)} %bitcast.50, s32[]{:T(128)} %constant.107.clone.1), kind=kCustom, calls=%fused_computation.48 | custom fusion | bytes 2052 | tf_op jit(solution)/shard_map/scatter | solution.py:98
  97.4 3.0 %scatter_custom_fusion.2 = s32[512]{0:T(512)} fusion(s32[512]{0:T(512)S(1)} %bitcast.47, s32[512]{0:T(512)S(1)} %bitcast.49, s32[]{:T(128)} %constant.111.clone.1), kind=kCustom, calls=%fused_computation.46 | custom fusion | bytes 2052 | tf_op jit(solution)/shard_map/scatter | solution.py:103
  100.4 2.5 %all-to-all-done.1 = f32[16,8,4,256]{3,2,0,1:T(4,128)S(1)} async-done(((f32[16,8,4,256]{3,2,0,1:T(4,128)}), f32[16,8,4,256]{3,2,0,1:T(4,128)S(1)}, u32[]{:S(2)}, u32[]{:S(2)}) %all-to-all-start.1) | async-done | bytes 524320 | tf_op jit(solution)/shard_map/all_to_all | solution.py:58
  103.0 0.2 reshape.271
  103.2 3.0 %scatter_custom_fusion = f32[512,256]{1,0:T(8,128)} fusion(s32[512]{0:T(512)S(1)} %bitcast.48, f32[512,256]{1,0:T(8,128)S(1)} %reshape.271, f32[]{:T(128)} %constant.100.clone.1), kind=kCustom, calls=%fused_computation.16 | custom fusion | bytes 524292 | tf_op jit(solution)/shard_map/scatter | solution.py:93
  (29 shorter events, 0.5 us)
Async XLA Ops:
  46.8 7.9 %copy-start = (s32[1,512]{1,0:T(1,128)S(1)}, s32[1,512]{1,0:T(1,128)}, u32[]{:S(2)}) copy-start(s32[1,512]{1,0:T(1,128)} %param.8) | copy-start | bytes 6148
  56.4 9.2 %all-to-all-start.2 = ((f32[4,1,256]{2,1,0:T(1,128)}), f32[4,1,256]{2,1,0:T(1,128)S(1)}, u32[]{:S(2)}, u32[]{:S(2)}) async-start(f32[4,1,256]{2,1,0:T(1,128)} %reshape.312), calls=%async_computation.2 | async-start | bytes 8192 | tf_op jit(solution)/shard_map/all_to_all | solution.py:69
  65.6 16.0 %all-to-all-start = ((f32[16,8,4,256]{3,1,0,2:T(8,128)}), f32[16,8,4,256]{3,1,0,2:T(8,128)S(1)}, u32[]{:S(2)}, u32[]{:S(2)}) async-start(f32[16,8,4,256]{3,1,0,2:T(8,128)} %copy.60), calls=%async_computation | async-start | bytes 1048576 | tf_op jit(solution)/shard_map/all_to_all | solution.py:59
  81.6 8.2 %all-to-all-start.3 = ((f32[8,1,128]{2,1,0:T(1,128)}), f32[8,1,128]{2,1,0:T(1,128)S(1)}, u32[]{:S(2)}, u32[]{:S(2)}) async-start(f32[8,1,128]{2,1,0:T(1,128)} %reshape.314), calls=%async_computation.3 | async-start | bytes 8192 | tf_op jit(solution)/shard_map/all_to_all | solution.py:66
  89.8 13.2 %all-to-all-start.1 = ((f32[16,8,4,256]{3,2,0,1:T(4,128)}), f32[16,8,4,256]{3,2,0,1:T(4,128)S(1)}, u32[]{:S(2)}, u32[]{:S(2)}) async-start(f32[16,8,4,256]{3,2,0,1:T(4,128)} %copy.61), calls=%async_computation.1 | async-start | bytes 1048576 | tf_op jit(solution)/shard_map/all_to_all | solution.py:58
